TPU v7x, 32 devices: a whole 2x2x4 slice. The times are simulated.
32 devices in a mesh: tm: 4 (over x, core), space: 8 (over z, y).
Axes of the slice: x: 2, y: 2, z: 4, core: 2. Of those that a mesh axis runs over, the one named last changes fastest.
Arguments:
- iterate: float32 [64, 16, 3, 4096], P('space', 'tm'), may hold values from -6 to 6
- forcing: float32 [64, 16, 3, 4096], P('space', 'tm'), may hold values from -6 to 6
- initial_velocity: float32 [64, 3, 4096], P('space'), may hold values from -6 to 6
- viscosity: float32 [64, 4096], P('space'), may hold values from 0.1 to 1
- peclet: float32 [64, 3, 4096], P('space'), may hold values from -0.9 to 0.9
- live_patch_mask: int32 [64], P('space'), may hold values from 0 to 1, as said below
- neighbour_holder: int32 [64, 6], P('space'), may hold values from -1 to 7, as said below
- neighbour_slot: int32 [64, 6], P('space'), may hold values from -1 to 7, as said below
Outputs:
- corrected_velocity: float32 [64, 16, 3, 4096], P('space', 'tm')
- corrected_residual: float32 [64, 16, 3, 4096], P('space', 'tm')
Inputs may be any that keep to these rules, and one draw needn't show every extreme that they name: `live_patch_mask`: on each index of space the live slots (1) come first; their count is 2 to 8, and in every draw some two indices j and j + 4 have all 8 slots live. `neighbour_holder`: the patches of one index s of space are the blocks of one aligned 2x2x2 octant; the octant's position is read from the bits of s: bit b of s is bit b div 3 of coordinate b mod 3, except that where a coordinate has two bits its lower bit is complemented when its higher bit is 1; slot p lies at offsets (p mod 2, p div 2 mod 2, p div 4); the entry is -1 where no live patch lies across the face or the slot is dead; the relation is symmetric across opposite faces; the live patches of one index face those of another given index across at most 4 faces, exactly 4 for some pair in every draw. `neighbour_slot`: -1 exactly where neighbour_holder is -1.
All inputs are finite; a program needn't handle non-finite values.
Results may differ from a plain program's by a relative error of at most 0.0003.
Values sent between devices are 32-bit elements; how exact they have to be, the bound alone decides.
A program may use at most 192 MiB of HBM per device.

v0:
```python
import jax
import jax.numpy as jnp
from jax import lax
from jax.sharding import PartitionSpec as P

WINDOW_SLICES = 16
BLOCK_EDGE = 16
SWEEPS = 5
FCAP = 4


STEP_DURATION = 0.5
ALPHA_SCALE = 0.1
HIGHEST_PRECISION = lax.Precision.HIGHEST


def shifted(value, axis, steps):
    count = lax.axis_size(axis)
    initial, last = (max(0, -steps), min(count, count - steps))
    return lax.ppermute(value, axis, [(source, source + steps) for source in range(initial, last)])


def face_masks(place_count):
    levels = place_count.bit_length() - 1
    return [[bit_index] for bit_index in range(levels)]


def face_routes(neighbour_holder, neighbour_slot, peer_ids, own_index):
    owners = neighbour_holder.reshape(-1)
    slot_numbers = neighbour_slot.reshape(-1)
    face_total = owners.shape[0]
    block_count = peer_ids.shape[0]
    face_codes = jnp.arange(face_total, dtype=jnp.int32)
    face_side = face_codes % 6
    across = jnp.maximum(slot_numbers, 0) * 6 + face_side + 1 - 2 * (face_side % 2)
    remote = (owners >= 0) & (owners != own_index)
    same_peer = remote[:, None] & remote[None, :] & (owners[:, None] == owners[None, :])
    send_rank = jnp.sum(same_peer & (across[None, :] < across[:, None]), axis=1)
    arrive_rank = jnp.sum(same_peer & (face_codes[None, :] < face_codes[:, None]), axis=1)
    matched = remote[:, None] & (owners[:, None] == peer_ids[None, :])
    block_ids = jnp.arange(block_count, dtype=jnp.int32)
    block_of = jnp.sum(jnp.where(matched, block_ids[None, :], 0), axis=1)
    covered = jnp.any(matched, axis=1)
    targets = jnp.arange(block_count * FCAP, dtype=jnp.int32)
    send_pick = (
        covered[None, :] & (block_of[None, :] * FCAP + send_rank[None, :] == targets[:, None])
    ).astype(jnp.float32)
    column = jnp.where(remote, block_of * FCAP + arrive_rank, block_count * FCAP + across)
    present = owners >= 0
    columns = jnp.arange(block_count * FCAP + face_total, dtype=jnp.int32)
    collect_pick = (present[:, None] & (column[:, None] == columns[None, :])).astype(jnp.float32)
    return (send_pick, collect_pick)


def neighbour_faces(flat_field, exchange_paths):
    send_pick, collect_pick, mask_list = exchange_paths
    slot_count, channels, cell_count = flat_field.shape
    width = channels * BLOCK_EDGE * BLOCK_EDGE
    cube_view = flat_field.reshape(slot_count, channels, BLOCK_EDGE, BLOCK_EDGE, BLOCK_EDGE)
    layers = jnp.stack(
        [
            cube_view[:, :, 0],
            cube_view[:, :, -1],
            cube_view[:, :, :, 0],
            cube_view[:, :, :, -1],
            cube_view[:, :, :, :, 0],
            cube_view[:, :, :, :, -1],
        ],
        axis=1,
    )
    layers = layers.reshape(slot_count * 6, width)
    outgoing = jnp.dot(send_pick, layers, precision=HIGHEST_PRECISION).reshape(-1, FCAP, width)
    incoming = lax.all_to_all(outgoing, "space", split_axis=0, concat_axis=0, tiled=True)
    sources = jnp.concatenate([incoming.reshape(-1, width), layers], axis=0)
    ghost_faces = jnp.dot(collect_pick, sources, precision=HIGHEST_PRECISION)
    return ghost_faces.reshape(slot_count, 6, channels, BLOCK_EDGE * BLOCK_EDGE)


def neighbour_sum(flat_field, ghost_faces, peclet):
    slot_count, channels, cell_count = flat_field.shape
    face_cells = BLOCK_EDGE * BLOCK_EDGE
    cell_index = jnp.arange(cell_count, dtype=jnp.int32)
    second_coord = cell_index // BLOCK_EDGE % BLOCK_EDGE
    third_coord = cell_index % BLOCK_EDGE

    def spread_second(layer):
        return jnp.broadcast_to(
            layer.reshape(slot_count, channels, BLOCK_EDGE, 1, BLOCK_EDGE),
            (slot_count, channels, BLOCK_EDGE, BLOCK_EDGE, BLOCK_EDGE),
        ).reshape(slot_count, channels, cell_count)

    def spread_third(layer):
        return jnp.broadcast_to(
            layer.reshape(slot_count, channels, face_cells, 1),
            (slot_count, channels, face_cells, BLOCK_EDGE),
        ).reshape(slot_count, channels, cell_count)

    x_upper = jnp.concatenate([flat_field[:, :, face_cells:], ghost_faces[:, 1]], axis=2)
    x_lower = jnp.concatenate([ghost_faces[:, 0], flat_field[:, :, :-face_cells]], axis=2)
    y_upper = jnp.where(
        second_coord == BLOCK_EDGE - 1,
        spread_second(ghost_faces[:, 3]),
        jnp.roll(flat_field, -BLOCK_EDGE, axis=2),
    )
    y_lower = jnp.where(
        second_coord == 0,
        spread_second(ghost_faces[:, 2]),
        jnp.roll(flat_field, BLOCK_EDGE, axis=2),
    )
    z_upper = jnp.where(
        third_coord == BLOCK_EDGE - 1,
        spread_third(ghost_faces[:, 5]),
        jnp.roll(flat_field, -1, axis=2),
    )
    z_lower = jnp.where(
        third_coord == 0, spread_third(ghost_faces[:, 4]), jnp.roll(flat_field, 1, axis=2)
    )
    x_peclet = peclet[:, 0:1]
    y_peclet = peclet[:, 1:2]
    z_peclet = peclet[:, 2:3]
    summed = (1.0 - x_peclet) * x_upper + (1.0 + x_peclet) * x_lower
    summed = summed + (1.0 - y_peclet) * y_upper + (1.0 + y_peclet) * y_lower
    summed = summed + (1.0 - z_peclet) * z_upper + (1.0 + z_peclet) * z_lower
    return summed


def compute_residual(
    velocity_state, forcing, initial_velocity, viscosity, peclet, live_indicator, exchange_paths
):
    slot_count, local_slices, components, cell_count = velocity_state.shape
    final_slice = velocity_state[:, -1]
    earlier = shifted(final_slice, "tm", 1)
    earlier = jnp.where(lax.axis_index("tm") == 0, initial_velocity, earlier)
    prior_slice = jnp.concatenate([earlier[:, None], velocity_state[:, :-1]], axis=1)
    flat_field = velocity_state.reshape(slot_count, local_slices * components, cell_count)
    ghost_faces = neighbour_faces(flat_field, exchange_paths)
    adjacent_sum = neighbour_sum(flat_field, ghost_faces, peclet).reshape(velocity_state.shape)
    operator_result = viscosity[:, None, None, :] * (6.0 * velocity_state - adjacent_sum)
    return (
        forcing - (velocity_state - prior_slice) / STEP_DURATION - operator_result
    ) * live_indicator[:, None, None, None]


def spectral_tables():
    times = jnp.arange(WINDOW_SLICES, dtype=jnp.int32)
    groups = WINDOW_SLICES // 2
    modes = jnp.arange(groups, dtype=jnp.int32)
    product = modes[:, None] * times[None, :] % WINDOW_SLICES
    angles = 2.0 * jnp.pi * product.astype(jnp.float32) / WINDOW_SLICES
    ramp = times.astype(jnp.float32) / WINDOW_SLICES
    twisted = jnp.power(ALPHA_SCALE, ramp)
    untwisted = jnp.power(ALPHA_SCALE, -ramp) / WINDOW_SLICES
    cosine = jnp.cos(angles)
    sine = jnp.sin(angles)
    root = ALPHA_SCALE ** (1.0 / WINDOW_SLICES)
    mode_angle = 2.0 * jnp.pi * modes.astype(jnp.float32) / WINDOW_SLICES
    shift_a = (1.0 - root * jnp.cos(mode_angle)) / STEP_DURATION
    shift_imag = root * jnp.sin(mode_angle) / STEP_DURATION
    alternating = (1 - 2 * (times % 2)).astype(jnp.float32)
    first_mode = (modes == 0)[:, None]
    second_row = jnp.where(first_mode, alternating[None, :], -sine)
    forward = jnp.stack([cosine, second_row], axis=1) * twisted[None, None, :]
    doubled = jnp.where(first_mode, 1.0, 2.0)
    back_second = jnp.where(first_mode, alternating[None, :], -2.0 * sine)
    inverse = jnp.stack([(doubled * cosine).T, back_second.T], axis=2) * untwisted[:, None, None]
    shift_b = jnp.where(modes == 0, (1.0 + root) / STEP_DURATION, shift_a)
    shift_imag = jnp.where(modes == 0, 0.0, shift_imag)
    return (forward, inverse, shift_a, shift_b, shift_imag)


def time_blocks(values):
    return lax.all_to_all(values, "tm", split_axis=0, concat_axis=0, tiled=True)


def spectral_blocks(values):
    return lax.all_to_all(values, "tm", split_axis=0, concat_axis=0, tiled=True)


def body(
    iterate,
    forcing,
    initial_velocity,
    viscosity,
    peclet,
    live_patch_mask,
    neighbour_holder,
    neighbour_slot,
):
    time_devices = lax.axis_size("tm")
    place_count = lax.axis_size("space")
    own_place = lax.axis_index("space")
    mask_list = face_masks(place_count)
    peer_ids = jnp.arange(place_count, dtype=jnp.int32)
    send_pick, collect_pick = face_routes(neighbour_holder, neighbour_slot, peer_ids, own_place)
    exchange_paths = (send_pick, collect_pick, mask_list)
    live_indicator = live_patch_mask.astype(jnp.float32)
    slot_count, local_slices, components, cell_count = iterate.shape
    slot_lead = slot_count // time_devices
    residual_value = compute_residual(
        iterate, forcing, initial_velocity, viscosity, peclet, live_indicator, exchange_paths
    )
    forward, inverse, shift_a, shift_b, shift_imag = spectral_tables()
    per_device = forward.shape[0] // time_devices
    regrouped = time_blocks(
        residual_value.reshape(time_devices, slot_lead, local_slices, components, cell_count)
    )
    forward_table = forward.reshape(time_devices, per_device, 2, time_devices, local_slices)
    spectrum = jnp.einsum(
        "agrtj,tsjcx->asgrcx", forward_table, regrouped, precision=HIGHEST_PRECISION
    )
    spectrum = spectral_blocks(spectrum).reshape(slot_count, per_device, 2, components, cell_count)
    first_group = lax.axis_index("tm") * per_device

    def own_modes(values):
        return lax.dynamic_slice_in_dim(values, first_group, per_device).reshape(
            1, per_device, 1, 1
        )

    diffusion = 6.0 * viscosity[:, None, None, :]
    diag_a = own_modes(shift_a) + diffusion
    diag_b = own_modes(shift_b) + diffusion
    coupling = own_modes(shift_imag)
    determinant = diag_a * diag_b + coupling * coupling
    source_real = spectrum[:, :, 0]
    source_imag = spectrum[:, :, 1]
    total_real = source_real
    total_imag = source_imag
    correction = spectrum
    for sweep_index in range(SWEEPS):
        if sweep_index > 0:
            flat_field = correction.reshape(slot_count, per_device * 2 * components, cell_count)
            ghost_faces = neighbour_faces(flat_field, exchange_paths)
            adjacent_sum = neighbour_sum(flat_field, ghost_faces, peclet).reshape(correction.shape)
            total_real = source_real + viscosity[:, None, None, :] * adjacent_sum[:, :, 0]
            total_imag = source_imag + viscosity[:, None, None, :] * adjacent_sum[:, :, 1]
        real_component = (diag_b * total_real + coupling * total_imag) / determinant
        imaginary_component = (diag_a * total_imag - coupling * total_real) / determinant
        correction = jnp.stack([real_component, imaginary_component], axis=2)
    returned = spectral_blocks(
        correction.reshape(time_devices, slot_lead, per_device, 2, components, cell_count)
    )
    inverse_table = inverse.reshape(time_devices, local_slices, time_devices, per_device, 2)
    update = jnp.einsum("tjagr,asgrcx->tsjcx", inverse_table, returned, precision=HIGHEST_PRECISION)
    update = time_blocks(update).reshape(iterate.shape)
    corrected_velocity = iterate + update
    corrected_residual = compute_residual(
        corrected_velocity,
        forcing,
        initial_velocity,
        viscosity,
        peclet,
        live_indicator,
        exchange_paths,
    )
    return (corrected_velocity, corrected_residual)


def solution(mesh):
    return jax.shard_map(
        body,
        mesh=mesh,
        in_specs=(
            P("space", "tm", None, None),
            P("space", "tm", None, None),
            P("space", None, None),
            P("space", None),
            P("space", None, None),
            P("space"),
            P("space", None),
            P("space", None),
        ),
        out_specs=(P("space", "tm", None, None), P("space", "tm", None, None)),
        check_vma=False,
    )
```

profile of v0, /device:TPU:0, one launch (start us, length us, event | category | flops | bytes accessed | tf_op | source)
XLA Modules:
  0.0 1305.8 jit_solution(7236250363456896547)
XLA Ops:
  13.2 7.4 fusion.195
  20.6 21.4 %fusion.194 = (f32[8,12,16,16,1]{4,3,2,0,1:T(8,128)}, f32[8,12,16,16,1]{4,3,2,0,1:T(8,128)}) fusion(f32[8,12,16,16,16]{4,3,2,0,1:T(8,128)} %reshape_reshape.18), kind=kLoop, calls=%fused_computation.363 | loop fusion | bytes 393216 | tf_op jit(solution)/shard_map/slice | solution.py:67
  43.3 11.0 copy.1007
  54.4 11.0 copy.1008
  83.0 7.3 all-to-all-start
  119.9 12.0 reshape.820
  137.8 12.0 reshape.821
  149.9 7.3 broadcast_in_dim.341
  157.2 12.0 reshape.822
  169.2 7.3 broadcast_in_dim.344
  176.5 12.4 reshape.823
  189.2 7.9 fusion.3
  204.0 18.9 %all-to-all-done.1 = f32[4,2,4,3,4096]{4,2,3,1,0:T(4,128)S(1)} async-done(((f32[4,2,4,3,4096]{4,2,3,1,0:T(4,128)}), f32[4,2,4,3,4096]{4,2,3,1,0:T(4,128)S(1)}, u32[]{:S(2)}, u32[]{:S(2)}) %all-to-all-start.1) | async-done | bytes 1572896 | tf_op jit(solution)/shard_map/all_to_all | solution.py:172
  233.4 19.0 %all-to-all-done.2 = f32[4,2,2,2,3,4096]{5,3,2,4,1,0:T(2,128)S(1)} async-done(((f32[4,2,2,2,3,4096]{5,3,2,4,1,0:T(2,128)}), f32[4,2,2,2,3,4096]{5,3,2,4,1,0:T(2,128)S(1)}, u32[]{:S(2)}, u32[]{:S(2)}) %all-to-all-start.2) | async-done | bytes 1572896 | tf_op jit(solution)/shard_map/all_to_all | solution.py:176
  265.4 21.5 %fusion.191 = (f32[8,12,16,16,1]{4,3,2,0,1:T(8,128)}, f32[8,12,16,16,1]{4,3,2,0,1:T(8,128)}) fusion(f32[8,12,16,16,16]{4,3,2,0,1:T(8,128)} %reshape_reshape.19), kind=kLoop, calls=%fused_computation.360 | loop fusion | bytes 393216 | tf_op jit(solution)/shard_map/slice | solution.py:67
  289.6 7.5 fusion.192
  297.0 11.8 copy.1031
  310.9 11.8 copy.1032
  360.6 9.6 all-to-all-done.3
  380.6 12.0 reshape.830
  398.6 12.0 reshape.831
  410.6 7.3 broadcast_in_dim.356
  417.9 12.0 reshape.832
  429.9 7.3 broadcast_in_dim.359
  437.3 12.1 reshape.833
  465.2 21.5 %fusion.188 = (f32[8,12,16,16,1]{4,3,2,0,1:T(8,128)}, f32[8,12,16,16,1]{4,3,2,0,1:T(8,128)}) fusion(f32[8,12,16,16,16]{4,3,2,0,1:T(8,128)} %reshape_reshape.20), kind=kLoop, calls=%fused_computation.357 | loop fusion | bytes 393216 | tf_op jit(solution)/shard_map/slice | solution.py:67
  489.4 7.5 fusion.189
  496.8 11.8 copy.1047
  510.7 11.8 copy.1048
  558.9 9.3 all-to-all-done.4
  578.7 12.0 reshape.838
  596.6 12.0 reshape.839
  615.9 12.0 reshape.840
  635.3 12.1 reshape.841
  663.2 21.5 %fusion.185 = (f32[8,12,16,16,1]{4,3,2,0,1:T(8,128)}, f32[8,12,16,16,1]{4,3,2,0,1:T(8,128)}) fusion(f32[8,12,16,16,16]{4,3,2,0,1:T(8,128)} %reshape_reshape.21), kind=kLoop, calls=%fused_computation.354 | loop fusion | bytes 393216 | tf_op jit(solution)/shard_map/slice | solution.py:67
  687.3 7.5 fusion.186
  694.8 11.8 copy.1063
  708.7 11.8 copy.1064
  756.8 9.2 all-to-all-done.5
  776.5 12.0 reshape.846
  794.5 12.0 reshape.847
  813.8 12.0 reshape.848
  833.2 12.1 reshape.849
  861.1 21.5 %fusion.182 = (f32[8,12,16,16,1]{4,3,2,0,1:T(8,128)}, f32[8,12,16,16,1]{4,3,2,0,1:T(8,128)}) fusion(f32[8,12,16,16,16]{4,3,2,0,1:T(8,128)} %reshape_reshape.22), kind=kLoop, calls=%fused_computation.351 | loop fusion | bytes 393216 | tf_op jit(solution)/shard_map/slice | solution.py:67
  885.2 7.5 fusion.183
  892.7 11.8 copy.1079
  906.6 11.8 copy.1080
  954.7 9.3 all-to-all-done.6
  974.5 12.0 reshape.854
  992.4 12.0 reshape.855
  1011.7 12.0 reshape.856
  1031.1 12.1 reshape.857
  1061.2 19.3 %all-to-all-done.7 = f32[4,2,2,2,3,4096]{5,3,2,4,1,0:T(2,128)S(1)} async-done(((f32[4,2,2,2,3,4096]{5,3,2,4,1,0:T(2,128)}), f32[4,2,2,2,3,4096]{5,3,2,4,1,0:T(2,128)S(1)}, u32[]{:S(2)}, u32[]{:S(2)}) %all-to-all-start.7) | async-done | bytes 1572896 | tf_op jit(solution)/shard_map/all_to_all | solution.py:176
  1085.7 23.0 %all_to_all.50 = f32[4,2,4,3,4096]{4,2,3,1,0:T(4,128)S(1)} all-to-all(f32[4,2,4,3,4096]{4,2,3,1,0:T(4,128)S(1)} %bitcast.467), channel_id=1, replica_groups=mesh['tm'=4,'space'=8] {'tm'}, dimensions={0} | all-to-all | bytes 3145728 | tf_op jit(solution)/shard_map/all_to_all | solution.py:172
  1119.8 7.4 fusion.180
  1127.2 21.4 %fusion.179 = (f32[8,12,16,16,1]{4,3,2,0,1:T(8,128)}, f32[8,12,16,16,1]{4,3,2,0,1:T(8,128)}) fusion(f32[8,12,16,16,16]{4,3,2,0,1:T(8,128)} %reshape_reshape.23), kind=kLoop, calls=%fused_computation.348 | loop fusion | bytes 393216 | tf_op jit(solution)/shard_map/slice | solution.py:67
  1149.6 11.0 copy.1101
  1160.6 11.0 copy.1102
  1212.3 7.7 all-to-all-done.9
  1226.9 12.0 reshape.863
  1244.9 12.0 reshape.864
  1264.2 12.0 reshape.865
  1283.6 12.1 reshape.866
  1296.0 7.5 fusion.54
  (531 shorter events, 525.4 us)
Async XLA Ops:
  1.4 111.7 %copy-start.109 = (pred[48]{0:T(512)(128)(4,1)}, pred[48]{0:T(512)(128)(4,1)S(1)}, u32[]{:S(2)}) copy-start(pred[48]{0:T(512)(128)(4,1)S(1)} %get-tuple-element.175) | copy-start | bytes 148
  20.6 21.4 %copy-start.122 = (s32[8,6]{1,0:T(8,128)S(1)}, s32[8,6]{1,0:T(8,128)}, u32[]{:S(2)}) copy-start(s32[8,6]{1,0:T(8,128)} %param.15) | copy-start | bytes 580
  81.8 31.4 %copy-start.107 = (s32[48]{0:T(128)}, s32[48]{0:T(128)S(1)}, u32[]{:S(2)}) copy-start(s32[48]{0:T(128)S(1)} %get-tuple-element.177) | copy-start | bytes 580
  83.0 30.0 %all-to-all-start = ((f32[8,4,3072]{2,1,0:T(4,128)}), f32[8,4,3072]{2,1,0:T(4,128)S(1)}, u32[]{:S(2)}, u32[]{:S(2)}) async-start(f32[8,4,3072]{2,1,0:T(4,128)} %fusion.176), calls=%async_computation | async-start | bytes 786432 | tf_op jit(solution)/shard_map/all_to_all | solution.py:73
  91.1 20.1 %collective-permute-start = (f32[8,3,4096]{2,0,1:T(8,128)}, f32[8,3,4096]{2,0,1:T(8,128)}, u32[]{:S(2)}, u32[]{:S(2)}) collective-permute-start(f32[8,3,4096]{2,0,1:T(8,128)} %slice_bitcast_fusion.1), channel_id=1, source_target_pairs={{0,8},{8,16},{16,24},{1,9},{9,17},{17,25},{2,10},{10,18},{18,26},{... | collective-permute-start | bytes 1179656 | tf_op jit(solution)/shard_map/ppermute | solution.py:20
  102.1 86.9 %copy-start.12 = (f32[8,4096]{1,0:T(8,128)}, f32[8,4096]{1,0:T(8,128)S(1)}, u32[]{:S(2)}) copy-start(f32[8,4096]{1,0:T(8,128)S(1)} %get-tuple-element.163) | copy-start | bytes 393220
  102.1 86.9 %copy-start.18 = (f32[8,4096]{1,0:T(8,128)}, f32[8,4096]{1,0:T(8,128)S(1)}, u32[]{:S(2)}) copy-start(f32[8,4096]{1,0:T(8,128)S(1)} %get-tuple-element.164) | copy-start | bytes 393220
  102.1 86.9 %copy-start.24 = (f32[8,4096]{1,0:T(8,128)}, f32[8,4096]{1,0:T(8,128)S(1)}, u32[]{:S(2)}) copy-start(f32[8,4096]{1,0:T(8,128)S(1)} %get-tuple-element.165) | copy-start | bytes 393220
  102.1 86.9 %copy-start.30 = (f32[8,4096]{1,0:T(8,128)}, f32[8,4096]{1,0:T(8,128)S(1)}, u32[]{:S(2)}) copy-start(f32[8,4096]{1,0:T(8,128)S(1)} %get-tuple-element.166) | copy-start | bytes 393220
  102.2 86.9 %copy-start.36 = (f32[8,4096]{1,0:T(8,128)}, f32[8,4096]{1,0:T(8,128)S(1)}, u32[]{:S(2)}) copy-start(f32[8,4096]{1,0:T(8,128)S(1)} %get-tuple-element.167) | copy-start | bytes 393220
  176.5 12.6 copy-start
  176.5 12.6 copy-start.42
  176.5 12.6 copy-start.75
  176.5 12.6 copy-start.78
  176.5 12.6 copy-start.84
  176.5 12.6 copy-start.85
  176.5 12.6 copy-start.89
  176.5 12.6 copy-start.90
  176.5 12.6 copy-start.123
  199.3 23.6 %copy-start.125 = (f32[4,4]{1,0:T(4,128)S(1)}, f32[4,4]{1,0:T(4,128)}, u32[]{:S(2)}) copy-start(f32[4,4]{1,0:T(4,128)} %fusion.153) | copy-start | bytes 196
  199.3 23.6 %all-to-all-start.1 = ((f32[4,2,4,3,4096]{4,2,3,1,0:T(4,128)}), f32[4,2,4,3,4096]{4,2,3,1,0:T(4,128)S(1)}, u32[]{:S(2)}, u32[]{:S(2)}) async-start(f32[4,2,4,3,4096]{4,2,3,1,0:T(4,128)} %bitcast.29), calls=%async_computation.1 | async-start | bytes 3145728 | tf_op jit(solution)/shard_map/all_to_all | solution.py:172
  228.2 24.1 %all-to-all-start.2 = ((f32[4,2,2,2,3,4096]{5,3,2,4,1,0:T(2,128)}), f32[4,2,2,2,3,4096]{5,3,2,4,1,0:T(2,128)S(1)}, u32[]{:S(2)}, u32[]{:S(2)}) async-start(f32[4,2,2,2,3,4096]{5,3,2,4,1,0:T(2,128)} %copy.1023), calls=%async_computation.2 | async-start | bytes 3145728 | tf_op jit(solution)/shard_map/all_to_all | solution.py:176
  233.3 23.7 %copy-start.2 = (f32[8,2,4096]{2,0,1:T(8,128)}, f32[8,2,4096]{2,0,1:T(8,128)S(1)}, u32[]{:S(2)}) copy-start(f32[8,2,4096]{2,0,1:T(8,128)S(1)} %get-tuple-element.169) | copy-start | bytes 786436
  233.4 23.7 %copy-start.7 = (f32[8,2,4096]{2,0,1:T(8,128)}, f32[8,2,4096]{2,0,1:T(8,128)S(1)}, u32[]{:S(2)}) copy-start(f32[8,2,4096]{2,0,1:T(8,128)S(1)} %get-tuple-element.170) | copy-start | bytes 786436
  352.6 17.5 %all-to-all-start.3 = ((f32[8,4,3072]{2,1,0:T(4,128)}), f32[8,4,3072]{2,1,0:T(4,128)}, u32[]{:S(2)}, u32[]{:S(2)}) async-start(f32[8,4,3072]{2,1,0:T(4,128)} %fusion.174), calls=%async_computation.3 | async-start | bytes 786432 | tf_op jit(solution)/shard_map/all_to_all | solution.py:73
  437.2 12.3 copy-start.37
  437.2 12.3 copy-start.79
  437.2 12.3 copy-start.91
  437.3 12.3 copy-start.92
  437.3 12.3 copy-start.99
  437.3 12.3 copy-start.100
  552.4 15.7 %all-to-all-start.4 = ((f32[8,4,3072]{2,1,0:T(4,128)}), f32[8,4,3072]{2,1,0:T(4,128)}, u32[]{:S(2)}, u32[]{:S(2)}) async-start(f32[8,4,3072]{2,1,0:T(4,128)} %fusion.172), calls=%async_computation.4 | async-start | bytes 786432 | tf_op jit(solution)/shard_map/all_to_all | solution.py:73
  635.2 12.3 copy-start.38
  635.3 12.3 copy-start.80
  635.3 12.3 copy-start.93
  635.3 12.3 copy-start.94
  635.3 12.3 copy-start.101
  635.3 12.3 copy-start.102
  750.4 15.6 %all-to-all-start.5 = ((f32[8,4,3072]{2,1,0:T(4,128)}), f32[8,4,3072]{2,1,0:T(4,128)}, u32[]{:S(2)}, u32[]{:S(2)}) async-start(f32[8,4,3072]{2,1,0:T(4,128)} %fusion.170), calls=%async_computation.5 | async-start | bytes 786432 | tf_op jit(solution)/shard_map/all_to_all | solution.py:73
  833.1 12.3 copy-start.39
  833.1 12.3 copy-start.81
  833.1 12.3 copy-start.95
  833.1 12.3 copy-start.96
  833.2 12.3 copy-start.103
  833.2 12.3 copy-start.104
  948.3 15.7 %all-to-all-start.6 = ((f32[8,4,3072]{2,1,0:T(4,128)}), f32[8,4,3072]{2,1,0:T(4,128)}, u32[]{:S(2)}, u32[]{:S(2)}) async-start(f32[8,4,3072]{2,1,0:T(4,128)} %fusion.168), calls=%async_computation.6 | async-start | bytes 786432 | tf_op jit(solution)/shard_map/all_to_all | solution.py:73
  1057.0 23.6 %all-to-all-start.7 = ((f32[4,2,2,2,3,4096]{5,3,2,4,1,0:T(2,128)}), f32[4,2,2,2,3,4096]{5,3,2,4,1,0:T(2,128)S(1)}, u32[]{:S(2)}, u32[]{:S(2)}) async-start(f32[4,2,2,2,3,4096]{5,3,2,4,1,0:T(2,128)} %copy.1093), calls=%async_computation.7 | async-start | bytes 3145728 | tf_op jit(solution)/shard_map/all_to_all | solution.py:176
  1085.6 23.0 %copy-start.1 = (f32[8,4,3,4096]{3,1,2,0:T(4,128)S(1)}, f32[8,4,3,4096]{3,1,2,0:T(4,128)}, u32[]{:S(2)}) copy-start(f32[8,4,3,4096]{3,1,2,0:T(4,128)} %param.8) | copy-start | bytes 4718596
  1204.9 15.3 %copy-start.108 = (s32[48]{0:T(128)S(1)}, s32[48]{0:T(128)}, u32[]{:S(2)}) copy-start(s32[48]{0:T(128)} %copy-done.107) | copy-start | bytes 580
  1204.9 15.3 %copy-start.110 = (pred[48]{0:T(512)(128)(4,1)S(1)}, pred[48]{0:T(512)(128)(4,1)}, u32[]{:S(2)}) copy-start(pred[48]{0:T(512)(128)(4,1)} %copy-done.109) | copy-start | bytes 148
  1204.9 15.1 %all-to-all-start.9 = ((f32[8,4,3072]{2,1,0:T(4,128)}), f32[8,4,3072]{2,1,0:T(4,128)S(1)}, u32[]{:S(2)}, u32[]{:S(2)}) async-start(f32[8,4,3072]{2,1,0:T(4,128)} %fusion.166), calls=%async_computation.9 | async-start | bytes 786432 | tf_op jit(solution)/shard_map/all_to_all | solution.py:73
  1208.7 2.8 collective-permute-start.1
  1283.5 12.3 copy-start.17
  1283.5 12.4 copy-start.23
  1283.5 12.4 copy-start.29
  1283.5 12.4 copy-start.35
  1283.5 12.4 copy-start.41
  1283.5 12.4 copy-start.47
  1283.6 12.4 copy-start.74
  1283.6 12.4 copy-start.83
  1283.6 12.4 copy-start.86
  1283.6 12.4 copy-start.87
  1283.6 12.4 copy-start.88
  1283.6 12.4 copy-start.124
  (76 other events, 498.1 us)
where the time goes:
time: 1320 us; the launch traced here: 1310 us
  local copies, waits for them, and re-layouts  1050 us (80%)
  waiting for transfers between devices  102 us (8%)
  other arithmetic  62.8 us (5%)
  starting transfers between devices  45.5 us (3%)
  blocking collectives  23 us (2%)
  matrix products  22.5 us (2%)
    slice x12, local copies, waits for them, and re-layouts, neighbour_faces(): cube_view[:, :, :, :, -1]  198 us
    reshape x12, local copies, waits for them, and re-layouts, spread_third(): return jnp.broadcast_to(layer.reshape(slot_count, channels, face_cells, 1...  145 us
    reshape x12, local copies, waits for them, and re-layouts, spread_second(): return jnp.broadcast_to(layer.reshape(slot_count, channels, BLOCK_EDGE, 1...  144 us
    broadcast_in_dim x30, local copies, waits for them, and re-layouts, spread_third(): jnp.broadcast_to(layer.reshape(slot_count, channels, face_cells, 1), (slo...  88.4 us
    broadcast_in_dim x24, local copies, waits for them, and re-layouts, spread_second(): jnp.broadcast_to(layer.reshape(slot_count, channels, BLOCK_EDGE, 1, BLOCK...  74.2 us
    slice x6, local copies, waits for them, and re-layouts, neighbour_faces(): cube_view[:, :, :, :, 0]  69.2 us
    reshape x12, local copies, waits for them, and re-layouts, neighbour_faces(): layers = layers.reshape(slot_count * 6, width)  69 us
    unnamed x291, local copies, waits for them, and re-layouts  49.4 us
  transfers between devices with their start and end apart: 11, of which 9 were waited for; matrix products, arithmetic and copies ran while one was open for 3% of the time, Pallas kernels for 0%

commit v1 on v0

v1 whole, which is shorter than its diff:
```python
import functools
import math

import jax
import jax.numpy as jnp
from jax import lax
from jax.experimental import pallas as pl
from jax.experimental.pallas import tpu as pltpu
from jax.sharding import PartitionSpec as P

WINDOW_SLICES = 16
BLOCK_EDGE = 16
SWEEPS = 5
STEP_DURATION = 0.5
ALPHA_SCALE = 0.1

ROWS = 32
LANES = 128
PAD = 8
TALL = ROWS + 2 * PAD
COMPONENTS = 3
GROUP = 16


def tables():
    n = WINDOW_SLICES
    root = ALPHA_SCALE ** (1.0 / n)
    forward, inverse, diagonals, coupling = [], [[] for _ in range(n)], [], []
    for mode in range(n // 2):
        angle = [2.0 * math.pi * (mode * time % n) / n for time in range(n)]
        alternate = [1.0 - 2.0 * (time % 2) for time in range(n)]
        twist = [root**time for time in range(n)]
        first = [math.cos(angle[t]) * twist[t] for t in range(n)]
        second = [(alternate[t] if mode == 0 else -math.sin(angle[t])) * twist[t] for t in range(n)]
        forward += [first, second]
        for t in range(n):
            back = root ** (-t) / n
            scale = 1.0 if mode == 0 else 2.0
            inverse[t] += [
                scale * math.cos(angle[t]) * back,
                (alternate[t] if mode == 0 else -2.0 * math.sin(angle[t])) * back,
            ]
        real = (1.0 - root * math.cos(2.0 * math.pi * mode / n)) / STEP_DURATION
        diagonals.append((real, (1.0 + root) / STEP_DURATION if mode == 0 else real))
        coupling.append(0.0 if mode == 0 else root * math.sin(2.0 * math.pi * mode / n) / STEP_DURATION)
    return forward, inverse, diagonals, coupling


def insert_bit(rank, dim, bit):
    low = 1 << dim
    return rank // low * (2 * low) + bit * low + rank % low


def remove_bit(slot, dim):
    low = 1 << dim
    return slot // (2 * low) * low + slot % low


def kernel(
    dims,
    weights,
    iterate,
    forcing,
    initial,
    viscosity,
    peclet,
    out_velocity,
    out_residual,
    state,
    residual,
    gathered,
    first_term,
    fields,
    factor_a,
    factor_b,
    spread,
    update,
    previous,
    res_send,
    res_recv,
    sweep_send,
    sweep_recv,
    send_sem,
    recv_sem,
    local_sem,
):
    time_devices, levels, slots, local = dims
    lead = slots // time_devices
    lead_bits = lead.bit_length() - 1
    forward, inverse, diagonals, coupling = tables()
    me = lax.axis_index("tm")
    place = lax.axis_index("space")
    place_bit = [place // (1 << b) % 2 for b in range(levels)]
    rows = lax.broadcasted_iota(jnp.int32, (ROWS, LANES), 0)
    lanes = lax.broadcasted_iota(jnp.int32, (ROWS, LANES), 1)
    odd_row = rows % 2 == 1
    z_index = lanes % BLOCK_EDGE
    y_block = lanes // BLOCK_EDGE

    space_links = []
    for b in range(levels):
        dim = b % 3
        if b + 3 < levels:
            side = 1 - (place_bit[b] + place_bit[b + 3]) % 2
        else:
            side = 1 - place_bit[b]
        partner = place + (1 << b) * (1 - 2 * place_bit[b])
        space_links.append((dim, side, {"space": partner}, 1 + b // 3))
    time_links = []
    for b in range(time_devices.bit_length() - 1):
        bit = me // (1 << b) % 2
        partner = me + (1 << b) * (1 - 2 * bit)
        time_links.append((lead_bits + b, 1 - bit, {"tm": partner}, 0))
    sweep_links = []
    for dim, side, partner, source in space_links:
        if dim >= lead_bits:
            step = 1 << (dim - lead_bits)
            partner = {**partner, "tm": me + step * (1 - 2 * (me // step % 2))}
        sweep_links.append((dim, side, partner, source))
    diagonal = [link[2] for link in sweep_links if len(link[2]) > 1]
    sweep_links += time_links

    barrier = pltpu.get_barrier_semaphore()
    greet = [link[2] for link in space_links]
    greet += diagonal
    greet += [{"tm": lax.rem(me + j, time_devices)} for j in range(1, time_devices)]
    for target in greet:
        pl.semaphore_signal(barrier, inc=1, device_id=target, device_id_type=pl.DeviceIdType.MESH)
    pl.semaphore_wait(barrier, len(greet))

    taken = [0]

    def send(source, target, device):
        number = taken[0]
        taken[0] += 1
        copy = pltpu.make_async_remote_copy(
            src_ref=source,
            dst_ref=target,
            send_sem=send_sem.at[number],
            recv_sem=recv_sem.at[number],
            device_id=device,
            device_id_type=pl.DeviceIdType.MESH,
        )
        copy.start()
        return copy

    def pack(load, count, dim, side, store):
        if dim == 0:
            def put(i, carry):
                store(pl.ds(PAD + 2 * i, 2), load(i, PAD + 30 * side, 2))
                return carry
            lax.fori_loop(0, count, put, 0)
            return

        def gather(i, packed):
            if dim == 1:
                parity = i // 8
                value = load(i, PAD + side - parity, ROWS)
                value = pltpu.roll(value, (i % 8 * BLOCK_EDGE + 128 - 112 * side) % 128, 1)
                chosen = (y_block == i % 8) & (rows % 2 == parity)
            else:
                value = load(i, PAD, ROWS)
                value = pltpu.roll(value, (i + 128 - 15 * side) % 128, 1)
                chosen = z_index == i
            return jnp.where(chosen, value, packed)

        packed = lax.fori_loop(0, count, gather, jnp.zeros((ROWS, LANES), jnp.float32))
        store(pl.ds(PAD, ROWS), packed)

    def received(load, i, dim, side):
        if dim == 0:
            return load(PAD + 2 * i, 2)
        if dim == 1:
            value = load(PAD + i // 8 - side, ROWS)
            return pltpu.roll(value, (112 * (1 - side) + 128 - i % 8 * BLOCK_EDGE) % 128, 1)
        return pltpu.roll(load(PAD, ROWS), (15 * side + 128 - i) % 128, 1)

    def beside(load, dim, side):
        if dim == 0:
            return load(PAD + 30 * (1 - side), 2)
        if dim == 1:
            return load(PAD + 1 - 2 * side, ROWS)
        return pltpu.roll(load(PAD, ROWS), (128 - 15 + 30 * side) % 128, 1)

    def adjacent(field, slot, coefficients, ghosts):
        upper, lower = [None] * 3, [None] * 3
        for dim, value, source in ghosts:
            high = weights[slot, dim, source, 1] * value
            low = weights[slot, dim, source, 0] * value
            upper[dim] = high if upper[dim] is None else upper[dim] + high
            lower[dim] = low if lower[dim] is None else lower[dim] + low
        field[pl.ds(PAD + ROWS, 2), :] = upper[0]
        field[pl.ds(PAD - 2, 2), :] = lower[0]
        value = field[pl.ds(PAD, ROWS), :]
        total = coefficients[0] * field[pl.ds(PAD + 2, ROWS), :]
        total = total + coefficients[1] * field[pl.ds(PAD - 2, ROWS), :]
        y_up = jnp.where(odd_row, upper[1], field[pl.ds(PAD + 1, ROWS), :])
        y_up = pltpu.roll(jnp.where(y_block == 0, y_up, value), 112, 1)
        y_low = jnp.where(odd_row, field[pl.ds(PAD - 1, ROWS), :], lower[1])
        y_low = pltpu.roll(jnp.where(y_block == 7, y_low, value), 16, 1)
        total = total + coefficients[2] * y_up + coefficients[3] * y_low
        z_up = jnp.where(z_index == 15, upper[2], pltpu.roll(value, 127, 1))
        z_low = jnp.where(z_index == 0, lower[2], pltpu.roll(value, 1, 1))
        return value, total + coefficients[4] * z_up + coefficients[5] * z_low

    def coefficients_of(slot):
        result = []
        for dim in range(3):
            number = peclet[slot, dim]
            result += [1.0 - number, 1.0 + number]
        return result

    def state_channel(i):
        return i // local, i % local

    def start_residual(phase):
        copies = []
        shift = send(
            state.at[:, :, local - 1, pl.ds(PAD, ROWS), :],
            previous.at[phase],
            {"tm": lax.rem(me + 1, time_devices)},
        )
        for number, (dim, side, partner, source) in enumerate(space_links):
            def one_slot(rank, carry, dim=dim, side=side, number=number):
                slot = insert_bit(rank, dim, side)

                def load(i, offset, size):
                    c, j = state_channel(i)
                    return state[c, slot, j, pl.ds(offset, size), :]

                def store(where, value):
                    res_send[phase, number, rank, where, :] = value

                pack(load, COMPONENTS * local, dim, side, store)
                return carry

            lax.fori_loop(0, slots // 2, one_slot, 0)
            copies.append(send(res_send.at[phase, number], res_recv.at[phase, number], partner))
        return shift, copies

    def residual_of(phase, c, store):
        def one_slot(slot, carry):
            coefficients = coefficients_of(slot)
            thickness = viscosity[slot]
            live = weights[slot, 0, 0, 2]
            bits = [slot // (1 << dim) % 2 for dim in range(3)]
            for j in range(local):
                i = c * local + j
                ghosts = []
                for dim in range(3):
                    other = slot + (1 << dim) * (1 - 2 * bits[dim])
                    load = lambda offset, size, other=other, j=j: state[
                        c, other, j, pl.ds(offset, size), :
                    ]
                    ghosts.append((dim, beside(load, dim, 1 - bits[dim]), 0))
                for number, (dim, side, partner, source) in enumerate(space_links):
                    rank = remove_bit(slot, dim)
                    load = lambda offset, size, number=number, rank=rank: res_recv[
                        phase, number, rank, pl.ds(offset, size), :
                    ]
                    ghosts.append((dim, received(load, i, dim, side), source))
                value, total = adjacent(state.at[c, slot, j], slot, coefficients, ghosts)
                if j == 0:
                    earlier = jnp.where(me == 0, initial[c, :, slot, :], previous[phase, c, slot])
                else:
                    earlier = state[c, slot, j - 1, pl.ds(PAD, ROWS), :]
                answer = forcing[slot, c, :, j, :] - (value - earlier) / STEP_DURATION
                answer = (answer - thickness * (6.0 * value - total)) * live
                store(slot, j, answer)
            return carry

        lax.fori_loop(0, slots, one_slot, 0)

    def take(slot, carry):
        for j in range(local):
            for c in range(COMPONENTS):
                state[c, slot, j, pl.ds(PAD, ROWS), :] = iterate[slot, c, :, j, :]
        return carry

    lax.fori_loop(0, slots, take, 0)
    shift, copies = start_residual(0)
    pending = [*copies]

    def make_factors(p, carry):
        slot = me * lead + p
        diffusion = 6.0 * viscosity[slot]
        for mode in range(GROUP // 2):
            real, second = diagonals[mode]
            if mode == 0:
                factor_a[p, mode] = 1.0 / (real + diffusion)
                factor_b[p, mode] = 1.0 / (second + diffusion)
            else:
                diagonal = real + diffusion
                determinant = diagonal * diagonal + coupling[mode] * coupling[mode]
                factor_a[p, mode] = diagonal / determinant
                factor_b[p, mode] = coupling[mode] / determinant
        return carry

    lax.fori_loop(0, lead, make_factors, 0)

    shift.wait()
    for copy in copies:
        copy.wait_recv()

    def exchange_time(source, target, number):
        moved = []
        for j in range(1, time_devices):
            peer = lax.rem(me + j, time_devices)
            moved.append(send(source(peer), target, {"tm": peer}))
        own = pltpu.make_async_copy(source(me), target, local_sem.at[number])
        own.start()
        return moved, own

    arrivals = []
    for c in range(COMPONENTS):
        def keep(slot, j, value, c=c):
            residual[c, slot, j] = value

        residual_of(0, c, keep)
        arrivals.append(
            exchange_time(
                lambda peer, c=c: residual.at[c, pl.ds(peer * lead, lead)], gathered.at[c, me], c
            )
        )

    def start_sweep(turn, c):
        copies = []
        for number, (dim, side, partner, source) in enumerate(sweep_links):
            inside = dim < lead_bits
            count = lead // 2 if inside else lead

            def one_slot(rank, carry, dim=dim, side=side, number=number, inside=inside):
                p = insert_bit(rank, dim, side) if inside else rank

                def load(i, offset, size):
                    return fields[turn % 2, c, p, i, pl.ds(offset, size), :]

                def store(where, value):
                    sweep_send[turn, c, number, rank, where, :] = value

                pack(load, GROUP, dim, side, store)
                return carry

            lax.fori_loop(0, count, one_slot, 0)
            copies.append(
                send(
                    sweep_send.at[turn, c, number, pl.ds(0, count)],
                    sweep_recv.at[turn, c, number, pl.ds(0, count)],
                    partner,
                )
            )
        pending.extend(copies)
        return copies

    sweeps = []
    for c in range(COMPONENTS):
        moved, own = arrivals[c]
        for copy in moved:
            copy.wait_recv()
        own.wait()
        pending.extend(moved)

        def transform(step, carry, c=c):
            p, chunk = step // (ROWS // 8), step % (ROWS // 8)
            at = pl.multiple_of(chunk * 8, 8)
            times = [
                gathered[c, t, p, j, pl.ds(at, 8), :] for t in range(time_devices) for j in range(local)
            ]
            for mode in range(GROUP // 2):
                sums = []
                for row in (forward[2 * mode], forward[2 * mode + 1]):
                    total = row[0] * times[0]
                    for t in range(1, WINDOW_SLICES):
                        if abs(row[t]) > 1e-12:
                            total = total + row[t] * times[t]
                    sums.append(total)
                a = factor_a[p, mode, pl.ds(at, 8), :]
                b = factor_b[p, mode, pl.ds(at, 8), :]
                if mode == 0:
                    real, imag = a * sums[0], b * sums[1]
                else:
                    real, imag = a * sums[0] + b * sums[1], a * sums[1] - b * sums[0]
                for part, value in ((0, real), (1, imag)):
                    first_term[c, p, 2 * mode + part, pl.ds(at, 8), :] = value
                    fields[0, c, p, 2 * mode + part, pl.ds(PAD + at, 8), :] = value
            return carry

        lax.fori_loop(0, lead * (ROWS // 8), transform, 0)
        sweeps.append(start_sweep(0, c))

    returns = []
    for turn in range(SWEEPS - 1):
        for c in range(COMPONENTS):
            for copy in sweeps[c]:
                copy.wait_recv()

            def one_slot(p, carry, turn=turn, c=c):
                slot = me * lead + p
                coefficients = coefficients_of(slot)
                thickness = viscosity[slot]

                def one_channel(i):
                    ghosts = []
                    for dim in range(lead_bits):
                        bit = p // (1 << dim) % 2
                        other = p + (1 << dim) * (1 - 2 * bit)
                        load = lambda offset, size, other=other: fields[
                            turn % 2, c, other, i, pl.ds(offset, size), :
                        ]
                        ghosts.append((dim, beside(load, dim, 1 - bit), 0))
                    for number, (dim, side, partner, source) in enumerate(sweep_links):
                        rank = remove_bit(p, dim) if dim < lead_bits else p
                        load = lambda offset, size, number=number, rank=rank: sweep_recv[
                            turn, c, number, rank, pl.ds(offset, size), :
                        ]
                        ghosts.append((dim, received(load, i, dim, side), source))
                    _, total = adjacent(fields.at[turn % 2, c, p, i], slot, coefficients, ghosts)
                    return thickness * total

                def one_mode(mode, carry):
                    real = one_channel(2 * mode)
                    imag = one_channel(2 * mode + 1)
                    a, b = factor_a[p, mode], factor_b[p, mode]
                    packed = mode == 0
                    cross = jnp.where(packed, 0.0, b)
                    imag_factor = jnp.where(packed, b, a)
                    new_real = first_term[c, p, 2 * mode] + (a * real + cross * imag)
                    new_imag = first_term[c, p, 2 * mode + 1] + (imag_factor * imag - cross * real)
                    later = (turn + 1) % 2
                    fields[later, c, p, 2 * mode, pl.ds(PAD, ROWS), :] = new_real
                    fields[later, c, p, 2 * mode + 1, pl.ds(PAD, ROWS), :] = new_imag
                    return carry

                return lax.fori_loop(0, GROUP // 2, one_mode, carry)

            lax.fori_loop(0, lead, one_slot, 0)
            if turn < SWEEPS - 2:
                sweeps[c] = start_sweep(turn + 1, c)
                continue

            def back(step, carry, c=c):
                p, chunk = step // (ROWS // 8), step % (ROWS // 8)
                at = pl.multiple_of(chunk * 8, 8)
                modes = [
                    fields[(SWEEPS - 1) % 2, c, p, i, pl.ds(PAD + at, 8), :] for i in range(GROUP)
                ]
                for time in range(WINDOW_SLICES):
                    row = inverse[time]
                    total = row[0] * modes[0]
                    for i in range(1, GROUP):
                        if abs(row[i]) > 1e-12:
                            total = total + row[i] * modes[i]
                    spread[c, time // local, p, time % local, pl.ds(at, 8), :] = total
                return carry

            lax.fori_loop(0, lead * (ROWS // 8), back, 0)
            returns.append(
                exchange_time(
                    lambda peer, c=c: spread.at[c, peer],
                    update.at[c, pl.ds(me * lead, lead)],
                    COMPONENTS + c,
                )
            )

    for c in range(COMPONENTS):
        moved, own = returns[c]
        for copy in moved:
            copy.wait_recv()
        own.wait()
        pending.extend(moved)

        def correct(slot, carry, c=c):
            for j in range(local):
                value = state[c, slot, j, pl.ds(PAD, ROWS), :] + update[c, slot, j]
                state[c, slot, j, pl.ds(PAD, ROWS), :] = value
                out_velocity[slot, c, :, j, :] = value
            return carry

        lax.fori_loop(0, slots, correct, 0)

    shift, copies = start_residual(1)
    pending.extend(copies)
    for copy in copies:
        copy.wait_recv()
    shift.wait()
    for c in range(COMPONENTS):
        def give(slot, j, value, c=c):
            out_residual[slot, c, :, j, :] = value

        residual_of(1, c, give)
    for copy in pending:
        copy.wait_send()


def body(
    iterate,
    forcing,
    initial_velocity,
    viscosity,
    peclet,
    live_patch_mask,
    neighbour_holder,
    neighbour_slot,
):
    time_devices = lax.axis_size("tm")
    levels = lax.axis_size("space").bit_length() - 1
    slots, local = iterate.shape[:2]
    lead = slots // time_devices
    place = lax.axis_index("space")

    holder = neighbour_holder.reshape(slots, 3, 2)
    depth = 1 + max(1, (levels + 2) // 3)
    sources = []
    for source in range(depth):
        per_dim = []
        for dim in range(3):
            b = dim + 3 * (source - 1)
            if source == 0:
                found = holder[:, dim] == place
            elif b < levels:
                found = holder[:, dim] == (place ^ (1 << b))
            else:
                found = jnp.zeros((slots, 2), bool)
            per_dim.append(found)
        sources.append(jnp.stack(per_dim, axis=1))
    weights = jnp.stack(sources, axis=2).astype(jnp.float32)
    live = jnp.broadcast_to(
        live_patch_mask.astype(jnp.float32)[:, None, None, None], (slots, 3, depth, 1)
    )
    weights = jnp.concatenate([weights, live], axis=3)

    def by_rows(array):
        split = array.reshape(array.shape[:-1] + (ROWS, LANES))
        return split.transpose((0, 2, 3, 1, 4) if split.ndim == 5 else (1, 2, 0, 3))

    def whole(array):
        return array.transpose(0, 3, 1, 2, 4).reshape(slots, local, COMPONENTS, ROWS * LANES)

    time_bits = time_devices.bit_length() - 1
    links = levels + time_bits
    turns = SWEEPS - 1
    copies = 2 * (1 + levels) + 2 * COMPONENTS * (time_devices - 1) + turns * COMPONENTS * links
    f32 = jnp.float32
    blocks = (ROWS, LANES)
    tall = (TALL, LANES)
    result = jax.ShapeDtypeStruct((slots, COMPONENTS, ROWS, local, LANES), f32)
    velocity, residual = pl.pallas_call(
        functools.partial(kernel, (time_devices, levels, slots, local)),
        out_shape=(result, result),
        in_specs=[pl.BlockSpec(memory_space=pltpu.SMEM)]
        + [pl.BlockSpec(memory_space=pltpu.VMEM)] * 5,
        out_specs=[pl.BlockSpec(memory_space=pltpu.VMEM)] * 2,
        scratch_shapes=[
            pltpu.VMEM((COMPONENTS, slots, local) + tall, f32),
            pltpu.VMEM((COMPONENTS, slots, local) + blocks, f32),
            pltpu.VMEM((COMPONENTS, time_devices, lead, local) + blocks, f32),
            pltpu.VMEM((COMPONENTS, lead, GROUP) + blocks, f32),
            pltpu.VMEM((2, COMPONENTS, lead, GROUP) + tall, f32),
            pltpu.VMEM((lead, GROUP // 2) + blocks, f32),
            pltpu.VMEM((lead, GROUP // 2) + blocks, f32),
            pltpu.VMEM((COMPONENTS, time_devices, lead, local) + blocks, f32),
            pltpu.VMEM((COMPONENTS, slots, local) + blocks, f32),
            pltpu.VMEM((2, COMPONENTS, slots) + blocks, f32),
            pltpu.VMEM((2, levels, slots // 2) + tall, f32),
            pltpu.VMEM((2, levels, slots // 2) + tall, f32),
            pltpu.VMEM((turns, COMPONENTS, links, lead) + tall, f32),
            pltpu.VMEM((turns, COMPONENTS, links, lead) + tall, f32),
            pltpu.SemaphoreType.DMA((copies,)),
            pltpu.SemaphoreType.DMA((copies,)),
            pltpu.SemaphoreType.DMA((2 * COMPONENTS,)),
        ],
        compiler_params=pltpu.CompilerParams(
            collective_id=0, has_side_effects=True, vmem_limit_bytes=60 * 1024 * 1024
        ),
    )(
        weights,
        by_rows(iterate),
        by_rows(forcing),
        by_rows(initial_velocity),
        viscosity.reshape((slots,) + blocks),
        peclet.reshape((slots, 3) + blocks),
    )
    return whole(velocity), whole(residual)


def solution(mesh):
    return jax.shard_map(
        body,
        mesh=mesh,
        in_specs=(
            P("space", "tm", None, None),
            P("space", "tm", None, None),
            P("space", None, None),
            P("space", None),
            P("space", None, None),
            P("space"),
            P("space", None),
            P("space", None),
        ),
        out_specs=(P("space", "tm", None, None), P("space", "tm", None, None)),
        check_vma=False,
    )
```

time: 1320 us -> 226 us (0.17); the launches traced: 1310 us -> 225 us
  local copies, waits for them, and re-layouts: 1050 us -> 8.37 us
  Pallas kernels: 0 us -> 215 us
  waiting for transfers between devices: 102 us -> 0 us
  other arithmetic: 62.8 us -> 1.39 us
  starting transfers between devices: 45.5 us -> 0 us
  blocking collectives: 23 us -> 0 us
  matrix products: 22.5 us -> 0 us
    slice x87 -> x0, local copies, waits for them, and re-layouts: 383 us -> none  [the longest x12 198 us: neighbour_faces(): cube_view[:, :, :, :, -1]]
    reshape x49 -> x2, local copies, waits for them, and re-layouts: 364 us -> 0.78 us  [the longest x1 0.77 us: body(): peclet.reshape((slots, 3) + blocks)]
    pallas_call x0 -> x1, Pallas kernels: none -> 215 us  [body(): pl.pallas_call(functools.partial(kernel, (time_devices, levels, slots, lo...]
    broadcast_in_dim x54 -> x1, local copies, waits for them, and re-layouts: 163 us -> 0.07 us  [body(): jnp.broadcast_to(live_patch_mask.astype(jnp.float32)[:, None, None, None]...]
    all_to_all x9 -> x0, waiting for transfers between devices: 102 us -> none  [the longest x6 45.1 us: neighbour_faces(): lax.all_to_all(outgoing, 'space', split_axis=0, concat_axis=0, tiled=True)]
    another operation x19 -> x2, local copies, waits for them, and re-layouts: 79.6 us -> 0.01 us  [body(): sources.append(jnp.stack(per_dim, axis=1))]
    unnamed x291 -> x7, local copies, waits for them, and re-layouts: 49.4 us -> 7.38 us
    all_to_all x9 -> x0, starting transfers between devices: 41.9 us -> none  [the longest x6 30.7 us: neighbour_faces(): lax.all_to_all(outgoing, 'space', split_axis=0, concat_axis=0, tiled=True)]
  transfers between devices with their start and end apart: 11 -> 0, of which waited for: 9 -> 0; matrix products, arithmetic and copies ran while one was open for 3% -> 0% of each run, Pallas kernels for 0% -> 0%
where the time goes in v1:
time: 226 us; the launch traced here: 225 us
  Pallas kernels  215 us (95%)
  local copies, waits for them, and re-layouts  8.37 us (4%)
    pallas_call x1, Pallas kernels, body(): pl.pallas_call(functools.partial(kernel, (time_devices, levels, slots, lo...  215 us
    unnamed x7, local copies, waits for them, and re-layouts  7.38 us

profile of v1, /device:TPU:0, one launch (start us, length us, event | category | flops | bytes accessed | tf_op | source)
XLA Modules:
  0.0 225.1 jit_solution(7137067882759750938)
XLA Ops:
  0.6 0.7 convert_element_type.7
  1.3 0.8 copy.32
  2.2 0.1 copy.36
  2.3 0.1 broadcast_in_dim.2
  2.3 0.7 pad_maximum_fusion.weights
  3.0 1.6 copy.46
  4.6 1.1 copy.45
  5.7 0.8 copy.37.peclet
  6.5 214.7 %shard_map.86 = (f32[8,3,32,4,128]{4,3,2,1,0:T(4,128)}, f32[8,3,32,4,128]{4,3,2,1,0:T(4,128)}) custom-call(f32[8,3,2,3]{3,2,1,0:T(2,128)} %pad_maximum_fusion.weights, f32[8,3,32,4,128]{4,3,2,1,0:T(4,128)} %bitcast.38, f32[8,3,32,4,128]{4,3,2,1,0:T(4,128)} %bitcast.39, f32[3,32,8,128]{3,2,1,0:T(8,128)} %bitcast.42, f32[8,32,128]{2,1,0:T(8,128)} %bitcast.40, ...), custom_call_target="tpu_custom_call" | custom-call | tf_op jit(solution)/shard_map/pallas_call | solution.py:547
  221.2 0.0 copy-start
  221.2 2.8 %copy.51 = f32[8,4,3,4096]{3,1,2,0:T(4,128)} copy(f32[8,4,3,4096]{3,1,2,0:T(4,128)} %bitcast.36) | data formatting | bytes 3145728
  224.0 0.0 copy-done
  224.0 1.1 copy.52
  (7 shorter events, 0.1 us)
Async XLA Ops:
  221.2 2.8 %copy-start = (f32[8,3,32,4,128]{4,3,2,1,0:T(4,128)S(1)}, f32[8,3,32,4,128]{4,3,2,1,0:T(4,128)}, u32[]{:S(2)}) copy-start(f32[8,3,32,4,128]{4,3,2,1,0:T(4,128)} %get-tuple-element.5) | copy-start | bytes 4718596

commit v2 on v1

--- a/solution.py
+++ b/solution.py
@@ -70,7 +70,8 @@
     residual,
     gathered,
     first_term,
-    fields,
+    fields_even,
+    fields_odd,
     factor_a,
     factor_b,
     spread,
@@ -87,6 +88,7 @@
     time_devices, levels, slots, local = dims
     lead = slots // time_devices
     lead_bits = lead.bit_length() - 1
+    fields = (fields_even, fields_odd)
     forward, inverse, diagonals, coupling = tables()
     me = lax.axis_index("tm")
     place = lax.axis_index("space")
@@ -146,13 +148,12 @@
 
     def pack(load, count, dim, side, store):
         if dim == 0:
-            def put(i, carry):
-                store(pl.ds(PAD + 2 * i, 2), load(i, PAD + 30 * side, 2))
-                return carry
-            lax.fori_loop(0, count, put, 0)
+            values = [load(i, PAD + 30 * side, 2) for i in range(count)]
+            for i in range(count):
+                store(pl.ds(PAD + 2 * i, 2), values[i])
             return
-
-        def gather(i, packed):
+        packed = jnp.zeros((ROWS, LANES), jnp.float32)
+        for i in range(count):
             if dim == 1:
                 parity = i // 8
                 value = load(i, PAD + side - parity, ROWS)
@@ -162,9 +163,7 @@
                 value = load(i, PAD, ROWS)
                 value = pltpu.roll(value, (i + 128 - 15 * side) % 128, 1)
                 chosen = z_index == i
-            return jnp.where(chosen, value, packed)
-
-        packed = lax.fori_loop(0, count, gather, jnp.zeros((ROWS, LANES), jnp.float32))
+            packed = jnp.where(chosen, value, packed)
         store(pl.ds(PAD, ROWS), packed)
 
     def received(load, i, dim, side):
@@ -182,25 +181,44 @@
             return load(PAD + 1 - 2 * side, ROWS)
         return pltpu.roll(load(PAD, ROWS), (128 - 15 + 30 * side) % 128, 1)
 
-    def adjacent(field, slot, coefficients, ghosts):
-        upper, lower = [None] * 3, [None] * 3
-        for dim, value, source in ghosts:
-            high = weights[slot, dim, source, 1] * value
-            low = weights[slot, dim, source, 0] * value
-            upper[dim] = high if upper[dim] is None else upper[dim] + high
-            lower[dim] = low if lower[dim] is None else lower[dim] + low
-        field[pl.ds(PAD + ROWS, 2), :] = upper[0]
-        field[pl.ds(PAD - 2, 2), :] = lower[0]
+    def source_weights(slot, sources):
+        result = []
+        for dim, source in sources:
+            low, high = weights[slot, dim, source, 0], weights[slot, dim, source, 1]
+            if dim == 0:
+                result.append((low, high))
+            else:
+                upper = odd_row if dim == 1 else z_index == 15
+                result.append(jnp.where(upper, high, low))
+        return result
+
+    def fill_ends(channels, ghosts_of, weighted):
+        ends = []
+        for i in range(len(channels)):
+            low = high = None
+            for value, (low_weight, high_weight) in zip(ghosts_of(i), weighted):
+                low = low_weight * value if low is None else low + low_weight * value
+                high = high_weight * value if high is None else high + high_weight * value
+            ends.append((low, high))
+        for field, (low, high) in zip(channels, ends):
+            field[pl.ds(PAD - 2, 2), :] = low
+            field[pl.ds(PAD + ROWS, 2), :] = high
+
+    def adjacent(field, coefficients, ghosts):
+        beyond = [None] * 3
+        for dim, value, weight in ghosts:
+            term = value * weight
+            beyond[dim] = term if beyond[dim] is None else beyond[dim] + term
         value = field[pl.ds(PAD, ROWS), :]
         total = coefficients[0] * field[pl.ds(PAD + 2, ROWS), :]
         total = total + coefficients[1] * field[pl.ds(PAD - 2, ROWS), :]
-        y_up = jnp.where(odd_row, upper[1], field[pl.ds(PAD + 1, ROWS), :])
+        y_up = jnp.where(odd_row, beyond[1], field[pl.ds(PAD + 1, ROWS), :])
         y_up = pltpu.roll(jnp.where(y_block == 0, y_up, value), 112, 1)
-        y_low = jnp.where(odd_row, field[pl.ds(PAD - 1, ROWS), :], lower[1])
+        y_low = jnp.where(odd_row, field[pl.ds(PAD - 1, ROWS), :], beyond[1])
         y_low = pltpu.roll(jnp.where(y_block == 7, y_low, value), 16, 1)
         total = total + coefficients[2] * y_up + coefficients[3] * y_low
-        z_up = jnp.where(z_index == 15, upper[2], pltpu.roll(value, 127, 1))
-        z_low = jnp.where(z_index == 0, lower[2], pltpu.roll(value, 1, 1))
+        z_up = jnp.where(z_index == 15, beyond[2], pltpu.roll(value, 127, 1))
+        z_low = jnp.where(z_index == 0, beyond[2], pltpu.roll(value, 1, 1))
         return value, total + coefficients[4] * z_up + coefficients[5] * z_low
 
     def coefficients_of(slot):
@@ -244,22 +262,36 @@
             thickness = viscosity[slot]
             live = weights[slot, 0, 0, 2]
             bits = [slot // (1 << dim) % 2 for dim in range(3)]
-            for j in range(local):
+            sources = [(dim, 0) for dim in range(3)]
+            sources += [(dim, source) for dim, side, partner, source in space_links]
+            weighted = source_weights(slot, sources)
+
+            def ghosts_of(j, wanted):
                 i = c * local + j
-                ghosts = []
+                found = []
                 for dim in range(3):
+                    if dim not in wanted:
+                        continue
                     other = slot + (1 << dim) * (1 - 2 * bits[dim])
-                    load = lambda offset, size, other=other, j=j: state[
-                        c, other, j, pl.ds(offset, size), :
-                    ]
-                    ghosts.append((dim, beside(load, dim, 1 - bits[dim]), 0))
+                    load = lambda offset, size: state[c, other, j, pl.ds(offset, size), :]
+                    found.append((dim, beside(load, dim, 1 - bits[dim]), weighted[dim]))
                 for number, (dim, side, partner, source) in enumerate(space_links):
+                    if dim not in wanted:
+                        continue
                     rank = remove_bit(slot, dim)
-                    load = lambda offset, size, number=number, rank=rank: res_recv[
+                    load = lambda offset, size: res_recv[
                         phase, number, rank, pl.ds(offset, size), :
                     ]
-                    ghosts.append((dim, received(load, i, dim, side), source))
-                value, total = adjacent(state.at[c, slot, j], slot, coefficients, ghosts)
+                    found.append((dim, received(load, i, dim, side), weighted[3 + number]))
+                return found
+
+            fill_ends(
+                [state.at[c, slot, j] for j in range(local)],
+                lambda j: [value for _, value, _ in ghosts_of(j, (0,))],
+                [w for (dim, _), w in zip(sources, weighted) if dim == 0],
+            )
+            for j in range(local):
+                value, total = adjacent(state.at[c, slot, j], coefficients, ghosts_of(j, (1, 2)))
                 if j == 0:
                     earlier = jnp.where(me == 0, initial[c, :, slot, :], previous[phase, c, slot])
                 else:
@@ -333,7 +365,7 @@
                 p = insert_bit(rank, dim, side) if inside else rank
 
                 def load(i, offset, size):
-                    return fields[turn % 2, c, p, i, pl.ds(offset, size), :]
+                    return fields[turn % 2][c, p, i, pl.ds(offset, size), :]
 
                 def store(where, value):
                     sweep_send[turn, c, number, rank, where, :] = value
@@ -382,7 +414,7 @@
                     real, imag = a * sums[0] + b * sums[1], a * sums[1] - b * sums[0]
                 for part, value in ((0, real), (1, imag)):
                     first_term[c, p, 2 * mode + part, pl.ds(at, 8), :] = value
-                    fields[0, c, p, 2 * mode + part, pl.ds(PAD + at, 8), :] = value
+                    fields_even[c, p, 2 * mode + part, pl.ds(PAD + at, 8), :] = value
             return carry
 
         lax.fori_loop(0, lead * (ROWS // 8), transform, 0)
@@ -399,39 +431,53 @@
                 coefficients = coefficients_of(slot)
                 thickness = viscosity[slot]
 
-                def one_channel(i):
-                    ghosts = []
+                now, after = fields[turn % 2], fields[(turn + 1) % 2]
+                sources = [(dim, 0) for dim in range(lead_bits)]
+                sources += [(dim, source) for dim, side, partner, source in sweep_links]
+                weighted = source_weights(slot, sources)
+
+                def ghosts_of(i, wanted):
+                    found = []
                     for dim in range(lead_bits):
+                        if dim not in wanted:
+                            continue
                         bit = p // (1 << dim) % 2
                         other = p + (1 << dim) * (1 - 2 * bit)
-                        load = lambda offset, size, other=other: fields[
-                            turn % 2, c, other, i, pl.ds(offset, size), :
-                        ]
-                        ghosts.append((dim, beside(load, dim, 1 - bit), 0))
+                        load = lambda offset, size: now[c, other, i, pl.ds(offset, size), :]
+                        found.append((dim, beside(load, dim, 1 - bit), weighted[dim]))
                     for number, (dim, side, partner, source) in enumerate(sweep_links):
+                        if dim not in wanted:
+                            continue
                         rank = remove_bit(p, dim) if dim < lead_bits else p
-                        load = lambda offset, size, number=number, rank=rank: sweep_recv[
+                        load = lambda offset, size: sweep_recv[
                             turn, c, number, rank, pl.ds(offset, size), :
                         ]
-                        ghosts.append((dim, received(load, i, dim, side), source))
-                    _, total = adjacent(fields.at[turn % 2, c, p, i], slot, coefficients, ghosts)
+                        found.append((dim, received(load, i, dim, side), weighted[lead_bits + number]))
+                    return found
+
+                fill_ends(
+                    [now.at[c, p, i] for i in range(GROUP)],
+                    lambda i: [value for _, value, _ in ghosts_of(i, (0,))],
+                    [w for (dim, _), w in zip(sources, weighted) if dim == 0],
+                )
+
+                def one_channel(i):
+                    _, total = adjacent(now.at[c, p, i], coefficients, ghosts_of(i, (1, 2)))
                     return thickness * total
 
-                def one_mode(mode, carry):
+                for mode in range(GROUP // 2):
                     real = one_channel(2 * mode)
                     imag = one_channel(2 * mode + 1)
                     a, b = factor_a[p, mode], factor_b[p, mode]
-                    packed = mode == 0
-                    cross = jnp.where(packed, 0.0, b)
-                    imag_factor = jnp.where(packed, b, a)
-                    new_real = first_term[c, p, 2 * mode] + (a * real + cross * imag)
-                    new_imag = first_term[c, p, 2 * mode + 1] + (imag_factor * imag - cross * real)
-                    later = (turn + 1) % 2
-                    fields[later, c, p, 2 * mode, pl.ds(PAD, ROWS), :] = new_real
-                    fields[later, c, p, 2 * mode + 1, pl.ds(PAD, ROWS), :] = new_imag
-                    return carry
-
-                return lax.fori_loop(0, GROUP // 2, one_mode, carry)
+                    if mode == 0:
+                        real, imag = a * real, b * imag
+                    else:
+                        real, imag = a * real + b * imag, a * imag - b * real
+                    for part, change in ((0, real), (1, imag)):
+                        after[c, p, 2 * mode + part, pl.ds(PAD, ROWS), :] = (
+                            first_term[c, p, 2 * mode + part] + change
+                        )
+                return carry
 
             lax.fori_loop(0, lead, one_slot, 0)
             if turn < SWEEPS - 2:
@@ -442,7 +488,7 @@
                 p, chunk = step // (ROWS // 8), step % (ROWS // 8)
                 at = pl.multiple_of(chunk * 8, 8)
                 modes = [
-                    fields[(SWEEPS - 1) % 2, c, p, i, pl.ds(PAD + at, 8), :] for i in range(GROUP)
+                    fields[(SWEEPS - 1) % 2][c, p, i, pl.ds(PAD + at, 8), :] for i in range(GROUP)
                 ]
                 for time in range(WINDOW_SLICES):
                     row = inverse[time]
@@ -555,7 +601,8 @@
             pltpu.VMEM((COMPONENTS, slots, local) + blocks, f32),
             pltpu.VMEM((COMPONENTS, time_devices, lead, local) + blocks, f32),
             pltpu.VMEM((COMPONENTS, lead, GROUP) + blocks, f32),
-            pltpu.VMEM((2, COMPONENTS, lead, GROUP) + tall, f32),
+            pltpu.VMEM((COMPONENTS, lead, GROUP) + tall, f32),
+            pltpu.VMEM((COMPONENTS, lead, GROUP) + tall, f32),
             pltpu.VMEM((lead, GROUP // 2) + blocks, f32),
             pltpu.VMEM((lead, GROUP // 2) + blocks, f32),
             pltpu.VMEM((COMPONENTS, time_devices, lead, local) + blocks, f32),

time: 226 us -> 123 us (0.54)
  Pallas kernels: 215 us -> 112 us
    pallas_call x1, Pallas kernels: 215 us -> 112 us  [body(): pl.pallas_call(functools.partial(kernel, (time_devices, levels, slots, lo...]
where the time goes in v2:
time: 123 us
  Pallas kernels  112 us (91%)
  local copies, waits for them, and re-layouts  8.37 us (7%)
  other arithmetic  1.39 us (1%)
    pallas_call x1, Pallas kernels, body(): pl.pallas_call(functools.partial(kernel, (time_devices, levels, slots, lo...  112 us
    unnamed x7, local copies, waits for them, and re-layouts  7.38 us

profile of v2, /device:TPU:0, one launch (start us, length us, event | category | flops | bytes accessed | tf_op | source)
XLA Modules:
  0.0 122.9 jit_solution(15762428812786083070)
XLA Ops:
  0.6 0.7 convert_element_type.7
  1.3 0.8 copy.32
  2.2 0.1 copy.36
  2.3 0.1 broadcast_in_dim.2
  2.3 0.7 pad_maximum_fusion.weights
  3.0 1.6 %copy.46 = f32[1,8,32,128]{3,2,1,0:T(8,128)} copy(f32[1,8,32,128]{3,1,2,0:T(8,128)} %bitcast.43) | data formatting | bytes 262144
  4.6 1.1 copy.45
  5.7 0.8 copy.37.peclet
  6.5 112.4 %shard_map.86 = (f32[8,3,32,4,128]{4,3,2,1,0:T(4,128)}, f32[8,3,32,4,128]{4,3,2,1,0:T(4,128)}) custom-call(f32[8,3,2,3]{3,2,1,0:T(2,128)} %pad_maximum_fusion.weights, f32[8,3,32,4,128]{4,3,2,1,0:T(4,128)} %bitcast.38, f32[8,3,32,4,128]{4,3,2,1,0:T(4,128)} %bitcast.39, f32[3,32,8,128]{3,2,1,0:T(8,128)} %bitcast.42, f32[8,32,128]{2,1,0:T(8,128)} %bitcast.40, ...), custom_call_target="tpu_custom_call" | custom-call | tf_op jit(solution)/shard_map/pallas_call | solution.py:593
  118.9 0.0 copy-start
  118.9 2.8 %copy.51 = f32[8,4,3,4096]{3,1,2,0:T(4,128)} copy(f32[8,4,3,4096]{3,1,2,0:T(4,128)} %bitcast.36) | data formatting | bytes 3145728
  121.7 0.0 copy-done
  121.7 1.1 copy.52
  (7 shorter events, 0.1 us)
Async XLA Ops:
  118.9 2.8 %copy-start = (f32[8,3,32,4,128]{4,3,2,1,0:T(4,128)S(1)}, f32[8,3,32,4,128]{4,3,2,1,0:T(4,128)}, u32[]{:S(2)}) copy-start(f32[8,3,32,4,128]{4,3,2,1,0:T(4,128)} %get-tuple-element.5) | copy-start | bytes 4718596
